TPU v7x, 32 devices: a whole 2x2x4 slice. The times are simulated.
32 devices in a mesh: expert: 4 (over z), neuron: 8 (over y, x, core).
Axes of the slice: x: 2, y: 2, z: 4, core: 2. Of those that a mesh axis runs over, the one named last changes fastest.
Arguments:
- tokens: bfloat16 [256, 4096], P('neuron'), may hold values from -6 to 6
- route_logits: float32 [256, 2], replicated, may hold values from -6 to 6
- expert_ids: int32 [256, 2], replicated, may hold values from 0 to 3, all different within a row; in each aligned block of 256 rows (0 to 255, 256 to 511, ...) at most 128 rows name the same one
- block_live: int32 [4, 224], P('expert', 'neuron'), may hold values 0 or 1
- w_gate: bfloat16 [4, 4096, 14336], P('expert', None, 'neuron'), may hold values from -0.09375 to 0.09375
- w_up: bfloat16 [4, 4096, 14336], P('expert', None, 'neuron'), may hold values from -0.09375 to 0.09375
- w_down: bfloat16 [4, 14336, 4096], P('expert', 'neuron'), may hold values from -0.046875 to 0.046875
Outputs:
- mixed: bfloat16 [256, 4096], P('neuron')
Inputs may be any that keep to these rules, and one draw needn't show every extreme that they name: `expert_ids`: each token names two different experts; no expert is named by more than 128 tokens, a bound that some block reaches; every expert is named.
All inputs are finite; a program needn't handle non-finite values. No bound on the sum of `block_live` on one device may be relied on, other than what follows from the above.
Results may differ from a plain program's by a relative error of at most 0.0049.
Values may be sent and summed in bfloat16 or wider, within the bound.
A program may use at most 128 MiB of HBM per device.

v0:
```python
import jax
import jax.numpy as jnp
from jax import lax
from jax.sharding import PartitionSpec as P

BLK = 64


def routing(expert_ids, route_logits, expert, capacity):
    chosen = (expert_ids == expert).astype(jnp.int32)
    flat_hits = chosen.reshape(-1)
    before = (jnp.cumsum(flat_hits) - flat_hits).reshape(chosen.shape)
    slot_pair = jnp.where(chosen > 0, before, capacity)
    leading = jax.nn.sigmoid(route_logits[:, 0] - route_logits[:, 1])
    mix_gates = jnp.stack([leading, 1.0 - leading], axis=1)
    weight = jnp.sum(mix_gates * chosen.astype(jnp.float32), axis=1)
    slot_tok = jnp.min(slot_pair, axis=1)
    slot_index = lax.broadcasted_iota(jnp.int32, (capacity, expert_ids.shape[0]), 0)
    dispatch = (
        (slot_pair[None, :, 0] == slot_index) | (slot_pair[None, :, 1] == slot_index)
    ).astype(jnp.bfloat16)
    return (dispatch, slot_tok, weight)


def per_device(tokens, route_logits, expert_ids, block_live, w_gate, w_up, w_down):
    total_tokens = expert_ids.shape[0]
    capacity = total_tokens // 2
    expert = lax.axis_index("expert")
    dispatch, slot_tok, weight = routing(expert_ids, route_logits, expert, capacity)
    gathered = jnp.dot(
        dispatch,
        lax.all_gather(tokens, "neuron", axis=0, tiled=True),
        preferred_element_type=jnp.float32,
    ).astype(jnp.bfloat16)
    gate_val = jnp.dot(gathered, w_gate[0], preferred_element_type=jnp.float32)
    up_val = jnp.dot(gathered, w_up[0], preferred_element_type=jnp.float32)
    live = jnp.repeat(block_live[0].astype(jnp.float32), BLK)
    hidden = (jax.nn.silu(gate_val) * up_val * live[None, :]).astype(jnp.bfloat16)
    partial_value = jnp.dot(hidden, w_down[0], preferred_element_type=jnp.float32)
    picked = jnp.take(partial_value, jnp.minimum(slot_tok, capacity - 1), axis=0)
    weighted = weight[:, None] * picked
    own_part = lax.psum_scatter(weighted, "neuron", scatter_dimension=0, tiled=True)
    mixed = lax.psum(own_part, "expert")
    return mixed.astype(jnp.bfloat16)


def solution(mesh):
    placed = (
        P("neuron", None),
        P(),
        P(),
        P("expert", "neuron"),
        P("expert", None, "neuron"),
        P("expert", None, "neuron"),
        P("expert", "neuron", None),
    )
    return jax.shard_map(
        per_device, mesh=mesh, in_specs=placed, out_specs=P("neuron", None), check_vma=False
    )
```

profile of v0, /device:TPU:0, one launch (start us, length us, event | category | flops | bytes accessed | tf_op | source)
XLA Modules:
  0.0 162.3 jit_solution(13914430239259568634)
XLA Ops:
  6.5 0.7 all-gather.2.cloned.1.call-update
  7.3 0.0 reduce-scatter.2.cloned.1.call-start
  7.3 0.8 broadcast_subtract_fusion
  8.1 0.7 fusion.23
  8.8 0.1 copy.21
  8.9 0.1 reshape.51
  9.1 0.3 reduce-window.9
  9.4 0.1 slice.21
  9.5 0.1 reshape.52
  9.6 0.7 convert_bitcast_fusion
  10.3 0.1 broadcast_in_dim.20
  10.3 0.1 mul.32
  10.4 0.1 slice_reduce_fusion
  10.6 0.1 broadcast.55
  10.6 0.1 reshape.54
  10.7 0.1 copy.22
  10.9 28.9 %all-gather.2.cloned.1.call-done = bf16[256,4096]{1,0:T(8,128)(2,1)} async-done(((bf16[32,4096]{1,0:T(8,128)(2,1)}), bf16[256,4096]{1,0:T(8,128)(2,1)}) %all-gather.2.cloned.1.call-update) | async-done | bytes 2097168 | tf_op jit(solution)/shard_map/all_gather | solution.py:32
  39.8 2.0 %convolution_convert_fusion = bf16[128,4096]{1,0:T(8,128)(2,1)S(1)} fusion(bf16[256,4096]{1,0:T(8,128)(2,1)} %all-gather.2.cloned.1.call-done, s32[256]{0:T(256)S(1)} %bitcast.27, s32[256]{0:T(256)S(1)} %bitcast.26), kind=kOutput, calls=%fused_computation.7 | convolution fusion | flops 269058048 | bytes 3147776 | tf_op jit(solution)/shard_map/dot_general | solution.py:30
  41.8 8.2 %fusion.4 = f32[128,1792]{1,0:T(8,128)} fusion(bf16[128,4096]{1,0:T(8,128)(2,1)S(1)} %convolution_convert_fusion, bf16[1,4096,1792]{2,1,0:T(8,128)(2,1)} %param.11), kind=kOutput, calls=%fused_computation.5 | convolution fusion | flops 1879048192 | bytes 16646144 | tf_op jit(solution)/shard_map/dot_general | solution.py:35
  50.0 14.1 %fusion = f32[128,4096]{1,0:T(8,128)S(1)} fusion(bf16[1,1792,4096]{2,1,0:T(8,128)(2,1)} %param.13, bf16[128,4096]{1,0:T(8,128)(2,1)S(1)} %convolution_convert_fusion, bf16[1,4096,1792]{2,1,0:T(8,128)(2,1)} %param.12, f32[128,1792]{1,0:T(8,128)} %fusion.4, f32[1792]{0:T(1024)S(1)} %mul.32), kind=kOutput, calls=%fused_computation.1 | convolution fusion | flops 3759702016 | bytes 33430528 | tf_op jit(solution)/shard_map/dot_general | solution.py:39
  64.1 3.8 %gather_fusion = f32[256,4096]{1,0:T(8,128)} fusion(f32[128,4096]{1,0:T(8,128)S(1)} %fusion, s32[1024]{0:T(1024)S(1)} %pad_clamp_fusion), kind=kCustom, calls=%fused_computation | custom fusion | bytes 8389632 | tf_op jit(solution)/shard_map/jit(_take)/gather | solution.py:40
  67.9 4.9 %select_multiply_fusion = f32[256,4096]{1,0:T(8,128)} fusion(f32[256,4096]{1,0:T(8,128)} %gather_fusion, f32[256]{0:T(256)S(1)} %get-tuple-element.5, pred[256]{0:T(512)(128)(4,1)S(1)} %compare_and_fusion), kind=kLoop, calls=%fused_computation.8 | loop fusion | flops 2097152 | bytes 8389888 | tf_op jit(solution)/shard_map/mul | solution.py:41
  72.8 51.3 %reduce-scatter.2.cloned.1.call-done = f32[32,4096]{1,0:T(8,128)} async-done(((f32[256,4096]{1,0:T(8,128)}), f32[32,4096]{1,0:T(8,128)}) %reduce-scatter.2.cloned.1.call-update) | async-done | bytes 524304 | tf_op jit(solution)/shard_map/reduce_scatter | solution.py:42
  124.1 31.4 %all-reduce.1 = bf16[32,4096]{1,0:T(8,128)(2,1)} all-reduce(f32[32,4096]{1,0:T(8,128)} %reduce-scatter.2.cloned.1.call-done), channel_id=1, replica_groups=mesh['expert'=4,'neuron'=8] {'expert'}, use_global_device_ids=true, to_apply=%region_5.6 | all-reduce | flops 131072 | bytes 786432 | tf_op jit(solution)/shard_map/psum | solution.py:43
  (9 shorter events, 0.1 us)
Async XLA Ops:
  6.5 33.2 %all-gather.2.cloned.1.call-start = ((), (), s32[]{:S(2)}) async-start(), calls=%async_computation.1 | async-start | bytes 2359296 | tf_op jit(solution)/shard_map/all_gather | solution.py:32
  7.3 116.8 %reduce-scatter.2.cloned.1.call-start = ((), (), s32[]{:S(2)}) async-start(), calls=%async_computation.2 | async-start | bytes 4718592 | tf_op jit(solution)/shard_map/reduce_scatter | solution.py:42
Sparse Core Ops, SparseCore 0:
  9.2 30.5 all-gather.1
  72.9 51.1 reduce-scatter.1
where the time goes:
time: 163 us; the launch traced here: 162 us
  waiting for transfers between devices  80.9 us (50%)
  blocking collectives  31.4 us (19%)
  matrix products  24.3 us (15%)
  between operations  13.5 us (8%)
  other arithmetic  7.42 us (5%)
  local copies, waits for them, and re-layouts  4.83 us (3%)
    reduce_scatter x1, waiting for transfers between devices, per_device(): lax.psum_scatter(weighted, 'neuron', scatter_dimension=0, tiled=True)  51.3 us
    psum x1, blocking collectives, per_device(): mixed = lax.psum(own_part, 'expert')  31.4 us
    all_gather x1, waiting for transfers between devices, per_device(): lax.all_gather(tokens, 'neuron', axis=0, tiled=True)  28.9 us
    dot_general x1, matrix products, per_device(): jnp.dot(hidden, w_down[0], preferred_element_type=jnp.float32)  14.1 us
    dot_general x1, matrix products, per_device(): gate_val = jnp.dot(gathered, w_gate[0], preferred_element_type=jnp.float32)  8.18 us
    mul x1, other arithmetic, per_device(): weighted = weight[:, None] * picked  4.89 us
    gather x1, local copies, waits for them, and re-layouts, per_device(): jnp.take(partial_value, jnp.minimum(slot_tok, capacity - 1), axis=0)  3.82 us
  transfers between devices with their start and end apart: 2, of which 2 were waited for; matrix products, arithmetic and copies ran while one was open for 2% of the time, Pallas kernels for 0%

commit v1 on v0

--- a/solution.py
+++ b/solution.py
@@ -40,7 +40,8 @@
     picked = jnp.take(partial_value, jnp.minimum(slot_tok, capacity - 1), axis=0)
     weighted = weight[:, None] * picked
     own_part = lax.psum_scatter(weighted, "neuron", scatter_dimension=0, tiled=True)
-    mixed = lax.psum(own_part, "expert")
+    bind_sheets = lambda slab_in, axis_tag: jnp.sum(jax.lax.all_gather(slab_in, axis_tag), axis=0)
+    mixed = bind_sheets(own_part, "expert")
     return mixed.astype(jnp.bfloat16)
 
 

time: 163 us -> 181 us (1.11)
  waiting for transfers between devices: 80.9 us -> 128 us
  blocking collectives: 31.4 us -> 0 us
  other arithmetic: 7.42 us -> 9.9 us
    all_gather x0 -> x1, waiting for transfers between devices: none -> 47.2 us  [per_device(): jax.lax.all_gather(slab_in, axis_tag)]
    psum x1 -> x0, blocking collectives: 31.4 us -> none  [per_device(): mixed = lax.psum(own_part, 'expert')]
    reduce_sum x0 -> x1, other arithmetic: none -> 2.48 us  [per_device(): jnp.sum(jax.lax.all_gather(slab_in, axis_tag), axis=0)]
  transfers between devices with their start and end apart: 2 -> 3, of which waited for: 2 -> 3; matrix products, arithmetic and copies ran while one was open for 2% -> 2% of each run, Pallas kernels for 0% -> 0%
where the time goes in v1:
time: 181 us; the launch traced here: 180 us
  waiting for transfers between devices  128 us (71%)
  matrix products  24.3 us (13%)
  between operations  13.2 us (7%)
  other arithmetic  9.9 us (5%)
  local copies, waits for them, and re-layouts  4.83 us (3%)
    reduce_scatter x1, waiting for transfers between devices, per_device(): lax.psum_scatter(weighted, 'neuron', scatter_dimension=0, tiled=True)  51.2 us
    all_gather x1, waiting for transfers between devices, per_device(): jax.lax.all_gather(slab_in, axis_tag)  47.2 us
    all_gather x1, waiting for transfers between devices, per_device(): lax.all_gather(tokens, 'neuron', axis=0, tiled=True)  28.9 us
    dot_general x1, matrix products, per_device(): jnp.dot(hidden, w_down[0], preferred_element_type=jnp.float32)  14.1 us
    dot_general x1, matrix products, per_device(): gate_val = jnp.dot(gathered, w_gate[0], preferred_element_type=jnp.float32)  8.18 us
    mul x1, other arithmetic, per_device(): weighted = weight[:, None] * picked  4.89 us
    gather x1, local copies, waits for them, and re-layouts, per_device(): jnp.take(partial_value, jnp.minimum(slot_tok, capacity - 1), axis=0)  3.82 us
  transfers between devices with their start and end apart: 3, of which 3 were waited for; matrix products, arithmetic and copies ran while one was open for 2% of the time, Pallas kernels for 0%

profile of v1, /device:TPU:0, one launch (start us, length us, event | category | flops | bytes accessed | tf_op | source)
XLA Modules:
  0.0 180.4 jit_solution(16449406159779286116)
XLA Ops:
  6.5 0.7 all-gather.4.cloned.1.call-update
  7.3 0.8 broadcast_subtract_fusion
  8.1 0.7 fusion.23
  8.8 0.1 copy.21
  8.9 0.1 reshape.51
  9.1 0.3 reduce-window.9
  9.4 0.1 slice.21
  9.5 0.1 reshape.52
  9.6 0.7 convert_bitcast_fusion
  10.3 0.1 broadcast_in_dim.20
  10.3 0.1 mul.32
  10.4 0.1 slice_reduce_fusion
  10.6 0.1 broadcast.55
  10.6 0.1 reshape.54
  10.7 0.1 copy.22
  10.9 28.9 %all-gather.4.cloned.1.call-done = bf16[256,4096]{1,0:T(8,128)(2,1)} async-done(((bf16[32,4096]{1,0:T(8,128)(2,1)}), bf16[256,4096]{1,0:T(8,128)(2,1)}) %all-gather.4.cloned.1.call-update) | async-done | bytes 2097168 | tf_op jit(solution)/shard_map/all_gather | solution.py:32
  39.8 2.0 %convolution_convert_fusion = bf16[128,4096]{1,0:T(8,128)(2,1)S(1)} fusion(bf16[256,4096]{1,0:T(8,128)(2,1)} %all-gather.4.cloned.1.call-done, s32[256]{0:T(256)S(1)} %bitcast.29, s32[256]{0:T(256)S(1)} %bitcast.28), kind=kOutput, calls=%fused_computation.7 | convolution fusion | flops 269058048 | bytes 3147776 | tf_op jit(solution)/shard_map/dot_general | solution.py:30
  41.8 8.2 %fusion.4 = f32[128,1792]{1,0:T(8,128)} fusion(bf16[128,4096]{1,0:T(8,128)(2,1)S(1)} %convolution_convert_fusion, bf16[1,4096,1792]{2,1,0:T(8,128)(2,1)} %param.11), kind=kOutput, calls=%fused_computation.5 | convolution fusion | flops 1879048192 | bytes 16646144 | tf_op jit(solution)/shard_map/dot_general | solution.py:35
  50.0 14.1 %fusion = f32[128,4096]{1,0:T(8,128)S(1)} fusion(bf16[1,1792,4096]{2,1,0:T(8,128)(2,1)} %param.13, bf16[128,4096]{1,0:T(8,128)(2,1)S(1)} %convolution_convert_fusion, bf16[1,4096,1792]{2,1,0:T(8,128)(2,1)} %param.12, f32[128,1792]{1,0:T(8,128)} %fusion.4, f32[1792]{0:T(1024)S(1)} %mul.32), kind=kOutput, calls=%fused_computation.1 | convolution fusion | flops 3759702016 | bytes 33430528 | tf_op jit(solution)/shard_map/dot_general | solution.py:39
  64.1 3.8 %gather_fusion = f32[256,4096]{1,0:T(8,128)} fusion(f32[128,4096]{1,0:T(8,128)S(1)} %fusion, s32[1024]{0:T(1024)S(1)} %pad_clamp_fusion), kind=kCustom, calls=%fused_computation | custom fusion | bytes 8389632 | tf_op jit(solution)/shard_map/jit(_take)/gather | solution.py:40
  67.9 4.9 %select_multiply_fusion = f32[256,4096]{1,0:T(8,128)} fusion(f32[256,4096]{1,0:T(8,128)} %gather_fusion, f32[256]{0:T(256)S(1)} %get-tuple-element.5, pred[256]{0:T(512)(128)(4,1)S(1)} %compare_and_fusion), kind=kLoop, calls=%fused_computation.8 | loop fusion | flops 2097152 | bytes 8389888 | tf_op jit(solution)/shard_map/mul | solution.py:41
  72.9 51.2 %reduce-scatter.2.cloned.1.call-done = f32[32,4096]{1,0:T(8,128)} async-done(((f32[256,4096]{1,0:T(8,128)}), f32[32,4096]{1,0:T(8,128)}) %reduce-scatter.2.cloned.1.call-update) | async-done | bytes 524304 | tf_op jit(solution)/shard_map/reduce_scatter | solution.py:42
  124.1 47.2 %all-gather.6.cloned.1.call-done = f32[128,4096]{1,0:T(8,128)} async-done(((f32[32,4096]{1,0:T(8,128)}), f32[128,4096]{1,0:T(8,128)}) %all-gather.6.cloned.1.call-update) | async-done | bytes 2097168 | tf_op jit(solution)/shard_map/all_gather | solution.py:43
  171.4 2.5 %reduce_sum.19 = bf16[32,4096]{1,0:T(8,128)(2,1)} reduce(f32[4,32,4096]{2,1,0:T(8,128)} %bitcast.27, f32[]{:T(128)} %constant.15.clone.1), dimensions={0}, to_apply=%region_5.6 | reduce | flops 393216 | bytes 2359300 | tf_op jit(solution)/shard_map/reduce_sum | solution.py:43
  (12 shorter events, 0.2 us)
Async XLA Ops:
  6.5 33.2 %all-gather.4.cloned.1.call-start = ((), (), s32[]{:S(2)}) async-start(), calls=%async_computation.1 | async-start | bytes 2359296 | tf_op jit(solution)/shard_map/all_gather | solution.py:32
  7.3 116.8 %reduce-scatter.2.cloned.1.call-start = ((), (), s32[]{:S(2)}) async-start(), calls=%async_computation.2 | async-start | bytes 4718592 | tf_op jit(solution)/shard_map/reduce_scatter | solution.py:42
  72.8 98.5 %all-gather.6.cloned.1.call-start = ((), (), s32[]{:S(2)}) async-start(), calls=%async_computation.3 | async-start | bytes 2621440 | tf_op jit(solution)/shard_map/all_gather | solution.py:43
Sparse Core Ops, SparseCore 0:
  9.2 30.5 all-gather.3
  72.9 51.1 reduce-scatter.1
  125.7 45.6 all-gather.5
